TPU v7x, 128 devices: a whole 4x4x4 slice. The times are simulated.
128 devices in a mesh: hst: 2 (over core), row: 4 (over x), col: 16 (over z, y).
Axes of the slice: x: 4, y: 4, z: 4, core: 2. Of those that a mesh axis runs over, the one named last changes fastest.
Arguments:
- tables: bfloat16 [1024, 1024, 128], P(('hst', 'row', 'col')), may hold values from -6 to 6
- indices: int32 [1024, 2048, 4], P(('hst', 'row', 'col')), may hold values from 0 to 1023
- lengths: int32 [1024, 2048], P(('hst', 'row', 'col')), may hold values from 1 to 4, as said below
- table_slot: int32 [1024], replicated, may hold values from 0 to 1023, each once
- dense_feature: bfloat16 [2048, 128], P(('hst', 'row', 'col')), may hold values from -48 to 48
- left_proj: bfloat16 [128, 1025], replicated, may hold values from -0.1875 to 0.1875
- right_proj: bfloat16 [128, 1025], replicated, may hold values from -0.1875 to 0.1875
Outputs:
- interaction: bfloat16 [2048, 16384], P(('hst', 'row', 'col'))
Inputs may be any that keep to these rules, and one draw needn't show every extreme that they name: Each bag uses its first lengths ids; some bag holds 4 ids.
All inputs are finite; a program needn't handle non-finite values.
Results may differ from a plain program's by a relative error of at most 0.0063.
Values may be sent and summed in bfloat16 or wider, within the bound.
A program may use at most 64 MiB of HBM per device.

v0:
```python
import jax
import jax.numpy as jnp
from jax import lax
from jax.sharding import PartitionSpec as P


def pool_table(table, row_ids, bag_lens, bag_size):
    all_samples = row_ids.shape[0]
    table_rows = table.shape[0]
    feature_width = table.shape[1]
    block = 512
    row_iota = lax.broadcasted_iota(jnp.int32, (1, table_rows), 1)

    def one_block(items):
        block_ids, block_lens = items

        def add_ids(position, counts):
            chosen_ids = lax.dynamic_index_in_dim(block_ids, position, 1, keepdims=False)
            hit = (chosen_ids[:, None] == row_iota) & (position < block_lens)[:, None]
            return counts + hit.astype(jnp.bfloat16)

        counts = jnp.zeros((block, table_rows), jnp.bfloat16)
        counts = lax.fori_loop(0, bag_size, add_ids, counts)
        return jnp.dot(counts, table, preferred_element_type=jnp.float32).astype(jnp.bfloat16)

    grouped_ids = row_ids.reshape(all_samples // block, block, row_ids.shape[1])
    grouped_lens = bag_lens.reshape(all_samples // block, block)
    pooled = lax.map(one_block, (grouped_ids, grouped_lens))
    return pooled.reshape(all_samples, feature_width)


def shards(tables, indices, lengths, table_slot, dense_feature, left_proj, right_proj):
    tab_dev, all_samples, bag_size = indices.shape
    feature_width = tables.shape[2]
    devices = lax.axis_size(("hst", "row", "col"))
    own_samples = all_samples // devices
    proj_rows = left_proj.shape[0]
    tables_total = left_proj.shape[1] - 1
    pooled = lax.map(
        lambda items: pool_table(items[0], items[1], items[2], bag_size), (tables, indices, lengths)
    )
    blocks = pooled.reshape(tab_dev, devices, own_samples, feature_width)
    positions = jnp.arange(tables_total, dtype=jnp.int32)
    within = positions % tab_dev
    source = positions // tab_dev
    slot_here = source * tab_dev + within
    projections = jnp.concatenate([left_proj, right_proj], axis=0)
    selector = (table_slot[:, None] == slot_here[None, :]).astype(jnp.bfloat16)
    proj_here = jnp.dot(projections[:, 1:], selector, preferred_element_type=jnp.float32).astype(
        jnp.bfloat16
    )
    received = lax.all_to_all(
        blocks, ("hst", "row", "col"), split_axis=1, concat_axis=0, tiled=True
    )
    count = received.shape[2]
    flattened = received.reshape(tables_total, count * feature_width)
    mixed_all = jnp.dot(proj_here, flattened, preferred_element_type=jnp.float32)
    mixed_all = mixed_all.reshape(2 * proj_rows, count, feature_width)
    dense_column = projections[:, 0].astype(jnp.float32)
    mixed_all = mixed_all + dense_column[:, None, None] * dense_feature[None].astype(jnp.float32)
    mixed_all = mixed_all.astype(jnp.bfloat16)
    left_side = mixed_all[:proj_rows]
    right_side = mixed_all[proj_rows:]
    products = jnp.einsum("kbe,lbe->bkl", left_side, right_side, preferred_element_type=jnp.float32)
    products = products * (1.0 / feature_width)
    return products.reshape(own_samples, proj_rows * proj_rows).astype(jnp.bfloat16)


def solution(mesh):
    in_specs = (
        P(("hst", "row", "col"), None, None),
        P(("hst", "row", "col"), None, None),
        P(("hst", "row", "col"), None),
        P(),
        P(("hst", "row", "col"), None),
        P(),
        P(),
    )
    out_specs = P(("hst", "row", "col"), None)
    return jax.shard_map(shards, mesh=mesh, in_specs=in_specs, out_specs=out_specs, check_vma=False)
```

profile of v0, /device:TPU:34, one launch (start us, length us, event | category | flops | bytes accessed | tf_op | source)
XLA Modules:
  0.0 217.0 jit_solution(7283805805666844912)
XLA Ops:
  0.0 125.8 %while.38 = (s32[]{:T(128)}, bf16[8,2048,128]{2,1,0:T(8,128)(2,1)}, s32[8,2048,4]{1,2,0:T(4,128)}, s32[8,2048]{1,0:T(8,128)}, bf16[8,1024,128]{2,1,0:T(8,128)(2,...) while((s32[]{:T(128)}, bf16[8,2048,128]{2,1,0:T(8,128)(2,1)}, ...), condition=%wide.region_5.6_spmd, body=%wide.region_0.5_spmd.sunk | while | flops 138478080 | bytes 5248493 | solution.py:39
  2.6 12.3 %while.39 = (s32[]{:T(128)}, bf16[4,512,128]{2,1,0:T(8,128)(2,1)S(1)}, s32[4,512,4]{1,2,0:T(4,128)S(1)}, s32[4,512]{1,0:T(4,128)S(1)}, bf16[1024,128]{1,0:T(8,12...) while((s32[]{:T(128)}, bf16[4,512,128]{2,1,0:T(8,128)(2,1)S(1)}, ...), condition=%wide.region_4.4_spmd.clone, body=%wide.region_1.3_spmd.clone.sunk | while | flops 138478080 | bytes 3577112 | solution.py:28
  2.7 2.5 %while.40 = (s32[]{:T(128)}, bf16[512,1024]{1,0:T(8,128)(2,1)S(1)}, s32[512,4]{0,1:T(4,128)S(1)}, s32[1,1024]{1,0:T(1,128)S(1)}, s32[512]{0:T(512)S(1)}, /*index=5*/s32[]{:T(128)}, s32[]{:T(128)}) while((s32[]{:T(128)}, bf16[512,1024]{1,0:T(8,128)(2,1)S(1)}, s32[512,4]{0,1:T(4,128)S(1)}, s32[1,1024]{1,0:T(1,128)S(1)}, ...), condition=%wide.region_3.2_spmd.clone, body=%wide.region_2.1_spmd.clone.sunk | while | flops 4194819 | bytes 2110567 | solution.py:23
  5.8 2.5 %while.40 = (s32[]{:T(128)}, bf16[512,1024]{1,0:T(8,128)(2,1)S(1)}, s32[512,4]{0,1:T(4,128)S(1)}, s32[1,1024]{1,0:T(1,128)S(1)}, s32[512]{0:T(512)S(1)}, /*index=5*/s32[]{:T(128)}, s32[]{:T(128)}) while((s32[]{:T(128)}, bf16[512,1024]{1,0:T(8,128)(2,1)S(1)}, s32[512,4]{0,1:T(4,128)S(1)}, s32[1,1024]{1,0:T(1,128)S(1)}, ...), condition=%wide.region_3.2_spmd.clone, body=%wide.region_2.1_spmd.clone.sunk | while | flops 4194819 | bytes 2110567 | solution.py:23
  8.8 2.5 %while.40 = (s32[]{:T(128)}, bf16[512,1024]{1,0:T(8,128)(2,1)S(1)}, s32[512,4]{0,1:T(4,128)S(1)}, s32[1,1024]{1,0:T(1,128)S(1)}, s32[512]{0:T(512)S(1)}, /*index=5*/s32[]{:T(128)}, s32[]{:T(128)}) while((s32[]{:T(128)}, bf16[512,1024]{1,0:T(8,128)(2,1)S(1)}, s32[512,4]{0,1:T(4,128)S(1)}, s32[1,1024]{1,0:T(1,128)S(1)}, ...), condition=%wide.region_3.2_spmd.clone, body=%wide.region_2.1_spmd.clone.sunk | while | flops 4194819 | bytes 2110567 | solution.py:23
  11.9 2.5 %while.40 = (s32[]{:T(128)}, bf16[512,1024]{1,0:T(8,128)(2,1)S(1)}, s32[512,4]{0,1:T(4,128)S(1)}, s32[1,1024]{1,0:T(1,128)S(1)}, s32[512]{0:T(512)S(1)}, /*index=5*/s32[]{:T(128)}, s32[]{:T(128)}) while((s32[]{:T(128)}, bf16[512,1024]{1,0:T(8,128)(2,1)S(1)}, s32[512,4]{0,1:T(4,128)S(1)}, s32[1,1024]{1,0:T(1,128)S(1)}, ...), condition=%wide.region_3.2_spmd.clone, body=%wide.region_2.1_spmd.clone.sunk | while | flops 4194819 | bytes 2110567 | solution.py:23
  18.3 12.3 %while.39 = (s32[]{:T(128)}, bf16[4,512,128]{2,1,0:T(8,128)(2,1)S(1)}, s32[4,512,4]{1,2,0:T(4,128)S(1)}, s32[4,512]{1,0:T(4,128)S(1)}, bf16[1024,128]{1,0:T(8,12...) while((s32[]{:T(128)}, bf16[4,512,128]{2,1,0:T(8,128)(2,1)S(1)}, ...), condition=%wide.region_4.4_spmd.clone, body=%wide.region_1.3_spmd.clone.sunk | while | flops 138478080 | bytes 3577112 | solution.py:28
  18.4 2.5 %while.40 = (s32[]{:T(128)}, bf16[512,1024]{1,0:T(8,128)(2,1)S(1)}, s32[512,4]{0,1:T(4,128)S(1)}, s32[1,1024]{1,0:T(1,128)S(1)}, s32[512]{0:T(512)S(1)}, /*index=5*/s32[]{:T(128)}, s32[]{:T(128)}) while((s32[]{:T(128)}, bf16[512,1024]{1,0:T(8,128)(2,1)S(1)}, s32[512,4]{0,1:T(4,128)S(1)}, s32[1,1024]{1,0:T(1,128)S(1)}, ...), condition=%wide.region_3.2_spmd.clone, body=%wide.region_2.1_spmd.clone.sunk | while | flops 4194819 | bytes 2110567 | solution.py:23
  21.5 2.5 %while.40 = (s32[]{:T(128)}, bf16[512,1024]{1,0:T(8,128)(2,1)S(1)}, s32[512,4]{0,1:T(4,128)S(1)}, s32[1,1024]{1,0:T(1,128)S(1)}, s32[512]{0:T(512)S(1)}, /*index=5*/s32[]{:T(128)}, s32[]{:T(128)}) while((s32[]{:T(128)}, bf16[512,1024]{1,0:T(8,128)(2,1)S(1)}, s32[512,4]{0,1:T(4,128)S(1)}, s32[1,1024]{1,0:T(1,128)S(1)}, ...), condition=%wide.region_3.2_spmd.clone, body=%wide.region_2.1_spmd.clone.sunk | while | flops 4194819 | bytes 2110567 | solution.py:23
  27.6 2.5 %while.40 = (s32[]{:T(128)}, bf16[512,1024]{1,0:T(8,128)(2,1)S(1)}, s32[512,4]{0,1:T(4,128)S(1)}, s32[1,1024]{1,0:T(1,128)S(1)}, s32[512]{0:T(512)S(1)}, /*index=5*/s32[]{:T(128)}, s32[]{:T(128)}) while((s32[]{:T(128)}, bf16[512,1024]{1,0:T(8,128)(2,1)S(1)}, s32[512,4]{0,1:T(4,128)S(1)}, s32[1,1024]{1,0:T(1,128)S(1)}, ...), condition=%wide.region_3.2_spmd.clone, body=%wide.region_2.1_spmd.clone.sunk | while | flops 4194819 | bytes 2110567 | solution.py:23
  34.1 12.3 %while.39 = (s32[]{:T(128)}, bf16[4,512,128]{2,1,0:T(8,128)(2,1)S(1)}, s32[4,512,4]{1,2,0:T(4,128)S(1)}, s32[4,512]{1,0:T(4,128)S(1)}, bf16[1024,128]{1,0:T(8,12...) while((s32[]{:T(128)}, bf16[4,512,128]{2,1,0:T(8,128)(2,1)S(1)}, ...), condition=%wide.region_4.4_spmd.clone, body=%wide.region_1.3_spmd.clone.sunk | while | flops 138478080 | bytes 3577112 | solution.py:28
  34.1 2.5 %while.40 = (s32[]{:T(128)}, bf16[512,1024]{1,0:T(8,128)(2,1)S(1)}, s32[512,4]{0,1:T(4,128)S(1)}, s32[1,1024]{1,0:T(1,128)S(1)}, s32[512]{0:T(512)S(1)}, /*index=5*/s32[]{:T(128)}, s32[]{:T(128)}) while((s32[]{:T(128)}, bf16[512,1024]{1,0:T(8,128)(2,1)S(1)}, s32[512,4]{0,1:T(4,128)S(1)}, s32[1,1024]{1,0:T(1,128)S(1)}, ...), condition=%wide.region_3.2_spmd.clone, body=%wide.region_2.1_spmd.clone.sunk | while | flops 4194819 | bytes 2110567 | solution.py:23
  37.2 2.5 %while.40 = (s32[]{:T(128)}, bf16[512,1024]{1,0:T(8,128)(2,1)S(1)}, s32[512,4]{0,1:T(4,128)S(1)}, s32[1,1024]{1,0:T(1,128)S(1)}, s32[512]{0:T(512)S(1)}, /*index=5*/s32[]{:T(128)}, s32[]{:T(128)}) while((s32[]{:T(128)}, bf16[512,1024]{1,0:T(8,128)(2,1)S(1)}, s32[512,4]{0,1:T(4,128)S(1)}, s32[1,1024]{1,0:T(1,128)S(1)}, ...), condition=%wide.region_3.2_spmd.clone, body=%wide.region_2.1_spmd.clone.sunk | while | flops 4194819 | bytes 2110567 | solution.py:23
  40.3 2.5 %while.40 = (s32[]{:T(128)}, bf16[512,1024]{1,0:T(8,128)(2,1)S(1)}, s32[512,4]{0,1:T(4,128)S(1)}, s32[1,1024]{1,0:T(1,128)S(1)}, s32[512]{0:T(512)S(1)}, /*index=5*/s32[]{:T(128)}, s32[]{:T(128)}) while((s32[]{:T(128)}, bf16[512,1024]{1,0:T(8,128)(2,1)S(1)}, s32[512,4]{0,1:T(4,128)S(1)}, s32[1,1024]{1,0:T(1,128)S(1)}, ...), condition=%wide.region_3.2_spmd.clone, body=%wide.region_2.1_spmd.clone.sunk | while | flops 4194819 | bytes 2110567 | solution.py:23
  43.3 2.5 %while.40 = (s32[]{:T(128)}, bf16[512,1024]{1,0:T(8,128)(2,1)S(1)}, s32[512,4]{0,1:T(4,128)S(1)}, s32[1,1024]{1,0:T(1,128)S(1)}, s32[512]{0:T(512)S(1)}, /*index=5*/s32[]{:T(128)}, s32[]{:T(128)}) while((s32[]{:T(128)}, bf16[512,1024]{1,0:T(8,128)(2,1)S(1)}, s32[512,4]{0,1:T(4,128)S(1)}, s32[1,1024]{1,0:T(1,128)S(1)}, ...), condition=%wide.region_3.2_spmd.clone, body=%wide.region_2.1_spmd.clone.sunk | while | flops 4194819 | bytes 2110567 | solution.py:23
  49.8 12.3 %while.39 = (s32[]{:T(128)}, bf16[4,512,128]{2,1,0:T(8,128)(2,1)S(1)}, s32[4,512,4]{1,2,0:T(4,128)S(1)}, s32[4,512]{1,0:T(4,128)S(1)}, bf16[1024,128]{1,0:T(8,12...) while((s32[]{:T(128)}, bf16[4,512,128]{2,1,0:T(8,128)(2,1)S(1)}, ...), condition=%wide.region_4.4_spmd.clone, body=%wide.region_1.3_spmd.clone.sunk | while | flops 138478080 | bytes 3577112 | solution.py:28
  49.9 2.5 %while.40 = (s32[]{:T(128)}, bf16[512,1024]{1,0:T(8,128)(2,1)S(1)}, s32[512,4]{0,1:T(4,128)S(1)}, s32[1,1024]{1,0:T(1,128)S(1)}, s32[512]{0:T(512)S(1)}, /*index=5*/s32[]{:T(128)}, s32[]{:T(128)}) while((s32[]{:T(128)}, bf16[512,1024]{1,0:T(8,128)(2,1)S(1)}, s32[512,4]{0,1:T(4,128)S(1)}, s32[1,1024]{1,0:T(1,128)S(1)}, ...), condition=%wide.region_3.2_spmd.clone, body=%wide.region_2.1_spmd.clone.sunk | while | flops 4194819 | bytes 2110567 | solution.py:23
  59.1 2.5 %while.40 = (s32[]{:T(128)}, bf16[512,1024]{1,0:T(8,128)(2,1)S(1)}, s32[512,4]{0,1:T(4,128)S(1)}, s32[1,1024]{1,0:T(1,128)S(1)}, s32[512]{0:T(512)S(1)}, /*index=5*/s32[]{:T(128)}, s32[]{:T(128)}) while((s32[]{:T(128)}, bf16[512,1024]{1,0:T(8,128)(2,1)S(1)}, s32[512,4]{0,1:T(4,128)S(1)}, s32[1,1024]{1,0:T(1,128)S(1)}, ...), condition=%wide.region_3.2_spmd.clone, body=%wide.region_2.1_spmd.clone.sunk | while | flops 4194819 | bytes 2110567 | solution.py:23
  65.5 12.3 %while.39 = (s32[]{:T(128)}, bf16[4,512,128]{2,1,0:T(8,128)(2,1)S(1)}, s32[4,512,4]{1,2,0:T(4,128)S(1)}, s32[4,512]{1,0:T(4,128)S(1)}, bf16[1024,128]{1,0:T(8,12...) while((s32[]{:T(128)}, bf16[4,512,128]{2,1,0:T(8,128)(2,1)S(1)}, ...), condition=%wide.region_4.4_spmd.clone, body=%wide.region_1.3_spmd.clone.sunk | while | flops 138478080 | bytes 3577112 | solution.py:28
  65.6 2.5 %while.40 = (s32[]{:T(128)}, bf16[512,1024]{1,0:T(8,128)(2,1)S(1)}, s32[512,4]{0,1:T(4,128)S(1)}, s32[1,1024]{1,0:T(1,128)S(1)}, s32[512]{0:T(512)S(1)}, /*index=5*/s32[]{:T(128)}, s32[]{:T(128)}) while((s32[]{:T(128)}, bf16[512,1024]{1,0:T(8,128)(2,1)S(1)}, s32[512,4]{0,1:T(4,128)S(1)}, s32[1,1024]{1,0:T(1,128)S(1)}, ...), condition=%wide.region_3.2_spmd.clone, body=%wide.region_2.1_spmd.clone.sunk | while | flops 4194819 | bytes 2110567 | solution.py:23
  71.7 2.5 %while.40 = (s32[]{:T(128)}, bf16[512,1024]{1,0:T(8,128)(2,1)S(1)}, s32[512,4]{0,1:T(4,128)S(1)}, s32[1,1024]{1,0:T(1,128)S(1)}, s32[512]{0:T(512)S(1)}, /*index=5*/s32[]{:T(128)}, s32[]{:T(128)}) while((s32[]{:T(128)}, bf16[512,1024]{1,0:T(8,128)(2,1)S(1)}, s32[512,4]{0,1:T(4,128)S(1)}, s32[1,1024]{1,0:T(1,128)S(1)}, ...), condition=%wide.region_3.2_spmd.clone, body=%wide.region_2.1_spmd.clone.sunk | while | flops 4194819 | bytes 2110567 | solution.py:23
  74.8 2.5 %while.40 = (s32[]{:T(128)}, bf16[512,1024]{1,0:T(8,128)(2,1)S(1)}, s32[512,4]{0,1:T(4,128)S(1)}, s32[1,1024]{1,0:T(1,128)S(1)}, s32[512]{0:T(512)S(1)}, /*index=5*/s32[]{:T(128)}, s32[]{:T(128)}) while((s32[]{:T(128)}, bf16[512,1024]{1,0:T(8,128)(2,1)S(1)}, s32[512,4]{0,1:T(4,128)S(1)}, s32[1,1024]{1,0:T(1,128)S(1)}, ...), condition=%wide.region_3.2_spmd.clone, body=%wide.region_2.1_spmd.clone.sunk | while | flops 4194819 | bytes 2110567 | solution.py:23
  81.3 12.3 %while.39 = (s32[]{:T(128)}, bf16[4,512,128]{2,1,0:T(8,128)(2,1)S(1)}, s32[4,512,4]{1,2,0:T(4,128)S(1)}, s32[4,512]{1,0:T(4,128)S(1)}, bf16[1024,128]{1,0:T(8,12...) while((s32[]{:T(128)}, bf16[4,512,128]{2,1,0:T(8,128)(2,1)S(1)}, ...), condition=%wide.region_4.4_spmd.clone, body=%wide.region_1.3_spmd.clone.sunk | while | flops 138478080 | bytes 3577112 | solution.py:28
  87.5 2.5 %while.40 = (s32[]{:T(128)}, bf16[512,1024]{1,0:T(8,128)(2,1)S(1)}, s32[512,4]{0,1:T(4,128)S(1)}, s32[1,1024]{1,0:T(1,128)S(1)}, s32[512]{0:T(512)S(1)}, /*index=5*/s32[]{:T(128)}, s32[]{:T(128)}) while((s32[]{:T(128)}, bf16[512,1024]{1,0:T(8,128)(2,1)S(1)}, s32[512,4]{0,1:T(4,128)S(1)}, s32[1,1024]{1,0:T(1,128)S(1)}, ...), condition=%wide.region_3.2_spmd.clone, body=%wide.region_2.1_spmd.clone.sunk | while | flops 4194819 | bytes 2110567 | solution.py:23
  97.0 12.3 %while.39 = (s32[]{:T(128)}, bf16[4,512,128]{2,1,0:T(8,128)(2,1)S(1)}, s32[4,512,4]{1,2,0:T(4,128)S(1)}, s32[4,512]{1,0:T(4,128)S(1)}, bf16[1024,128]{1,0:T(8,12...) while((s32[]{:T(128)}, bf16[4,512,128]{2,1,0:T(8,128)(2,1)S(1)}, ...), condition=%wide.region_4.4_spmd.clone, body=%wide.region_1.3_spmd.clone.sunk | while | flops 138478080 | bytes 3577112 | solution.py:28
  112.7 12.3 %while.39 = (s32[]{:T(128)}, bf16[4,512,128]{2,1,0:T(8,128)(2,1)S(1)}, s32[4,512,4]{1,2,0:T(4,128)S(1)}, s32[4,512]{1,0:T(4,128)S(1)}, bf16[1024,128]{1,0:T(8,12...) while((s32[]{:T(128)}, bf16[4,512,128]{2,1,0:T(8,128)(2,1)S(1)}, ...), condition=%wide.region_4.4_spmd.clone, body=%wide.region_1.3_spmd.clone.sunk | while | flops 138478080 | bytes 3577112 | solution.py:28
  125.8 5.4 %copy.9 = bf16[8,128,16,128]{3,2,0,1:T(8,128)(2,1)} copy(bf16[8,128,16,128]{3,2,1,0:T(8,128)(2,1)} %bitcast.66) | data formatting | bytes 8388608 | tf_op jit(solution)/shard_map/reshape | solution.py:42
  131.2 10.7 %all-to-all-start = ((bf16[8,128,16,128]{3,2,0,1:T(8,128)(2,1)}), bf16[8,128,16,128]{3,2,0,1:T(8,128)(2,1)}, u32[]{:S(2)}, u32[]{:S(2)}) async-start(bf16[8,128,16,128]{3,2,0,1:T(8,128)(2,1)} %copy.9), calls=%async_computation | async-start | bytes 8388608 | tf_op jit(solution)/shard_map/all_to_all | solution.py:52
  142.1 56.2 %all-to-all-done = bf16[8,128,16,128]{3,2,0,1:T(8,128)(2,1)} async-done(((bf16[8,128,16,128]{3,2,0,1:T(8,128)(2,1)}), bf16[8,128,16,128]{3,2,0,1:T(8,128)(2,1)}, u32[]{:S(2)}, u32[]{:S(2)}) %all-to-all-start) | async-done | bytes 4194336 | tf_op jit(solution)/shard_map/all_to_all | solution.py:52
  198.3 6.3 %copy.15 = bf16[128,8,16,128]{3,1,2,0:T(8,128)(2,1)} copy(bf16[128,8,16,128]{3,2,1,0:T(8,128)(2,1)} %bitcast.18) | data formatting | bytes 8388608
  204.6 6.4 %copy.10 = bf16[2048,1024]{1,0:T(8,128)(2,1)} copy(bf16[2048,1024]{0,1:T(8,128)(2,1)} %bitcast.64) | data formatting | bytes 8388608 | tf_op jit(solution)/shard_map/dot_general | solution.py:57
  211.0 4.4 %add_convert_fusion = bf16[256,16,128]{2,0,1:T(8,128)(2,1)S(1)} fusion(bf16[16,128,1024]{2,1,0:T(8,128)(2,1)} %bitcast.67, f32[16,128]{1,0:T(8,128)S(1)} %convert_element_type.40, f32[256]{0:T(256)S(1)} %bitcast.70, s32[1024]{0:T(1024)S(1)} %fusion.29, s32[1024]{0:T(1024)S(1)} %copy-done.3, bf16[256,1025]{0,1:T(8,128)(2,1)S(1)} %constant_dynamic-update-slice_fusion), kind=kOutput, calls=%fused_computation.17 | convolution fusion | flops 1613496320 | bytes 5784576 | tf_op jit(solution)/shard_map/dot_general | solution.py:57
  (623 shorter events, 157.9 us)
Async XLA Ops:
  131.2 10.7 %copy-start.2 = (bf16[16,128]{1,0:T(8,128)(2,1)S(1)}, bf16[16,128]{1,0:T(8,128)(2,1)}, u32[]{:S(2)}) copy-start(bf16[16,128]{1,0:T(8,128)(2,1)} %param.17) | copy-start | bytes 12292
  131.2 10.7 %copy-start = (bf16[128,1025]{0,1:T(8,128)(2,1)S(1)}, bf16[128,1025]{0,1:T(8,128)(2,1)}, u32[]{:S(2)}) copy-start(bf16[128,1025]{0,1:T(8,128)(2,1)} %param.18) | copy-start | bytes 787204
  131.2 10.8 %copy-start.1 = (bf16[128,1025]{0,1:T(8,128)(2,1)S(1)}, bf16[128,1025]{0,1:T(8,128)(2,1)}, u32[]{:S(2)}) copy-start(bf16[128,1025]{0,1:T(8,128)(2,1)} %param.19) | copy-start | bytes 787204
  131.2 67.1 %all-to-all-start = ((bf16[8,128,16,128]{3,2,0,1:T(8,128)(2,1)}), bf16[8,128,16,128]{3,2,0,1:T(8,128)(2,1)}, u32[]{:S(2)}, u32[]{:S(2)}) async-start(bf16[8,128,16,128]{3,2,0,1:T(8,128)(2,1)} %copy.9), calls=%async_computation | async-start | bytes 8388608 | tf_op jit(solution)/shard_map/all_to_all | solution.py:52
  204.6 6.4 %copy-start.3 = (s32[1024]{0:T(1024)S(1)}, s32[1024]{0:T(1024)}, u32[]{:S(2)}) copy-start(s32[1024]{0:T(1024)} %param.16) | copy-start | bytes 12292
where the time goes:
time: 219 us; the launch traced here: 217 us
  other arithmetic  73.6 us (34%)
  waiting for transfers between devices  56.2 us (26%)
  local copies, waits for them, and re-layouts  48.8 us (22%)
  matrix products  20.5 us (9%)
  starting transfers between devices  10.7 us (5%)
  loops' own time  7.05 us (3%)
    add x128, other arithmetic, add_ids(): return counts + hit.astype(jnp.bfloat16)  72.8 us
    all_to_all x1, waiting for transfers between devices, shards(): lax.all_to_all(blocks, ('hst', 'row', 'col'), split_axis=1, concat_axis=0...  56.2 us
    dot_general x32, matrix products, one_block(): jnp.dot(counts, table, preferred_element_type=jnp.float32)  15.7 us
    dynamic_slice x16, local copies, waits for them, and re-layouts, shards(): lax.map(lambda items: pool_table(items[0], items[1], items[2], bag_size),...  13 us
    all_to_all x1, starting transfers between devices, shards(): lax.all_to_all(blocks, ('hst', 'row', 'col'), split_axis=1, concat_axis=0...  10.7 us
    squeeze x8, local copies, waits for them, and re-layouts, shards(): lax.map(lambda items: pool_table(items[0], items[1], items[2], bag_size),...  7.79 us
    unnamed x11, local copies, waits for them, and re-layouts  7.48 us
    dynamic_update_slice x8, local copies, waits for them, and re-layouts, shards(): lax.map(lambda items: pool_table(items[0], items[1], items[2], bag_size),...  6.71 us
  transfers between devices with their start and end apart: 1, of which 1 were waited for; matrix products, arithmetic and copies ran while one was open for 0% of the time, Pallas kernels for 0%

commit v1 on v0

--- a/solution.py
+++ b/solution.py
@@ -49,9 +49,11 @@
     proj_here = jnp.dot(projections[:, 1:], selector, preferred_element_type=jnp.float32).astype(
         jnp.bfloat16
     )
-    received = lax.all_to_all(
-        blocks, ("hst", "row", "col"), split_axis=1, concat_axis=0, tiled=True
-    )
+    v_next = lax.axis_size(("hst", "row", "col"))
+    z1 = jnp.split(blocks, v_next, axis=1)
+    row_out = jnp.stack(z1)
+    mat_out = lax.all_to_all(row_out, axis_name=("hst", "row", "col"), split_axis=0, concat_axis=0)
+    received = jnp.concatenate(mat_out, axis=0)
     count = received.shape[2]
     flattened = received.reshape(tables_total, count * feature_width)
     mixed_all = jnp.dot(proj_here, flattened, preferred_element_type=jnp.float32)

time: 219 us -> 344 us (1.57); the launches traced: 217 us -> 338 us
  local copies, waits for them, and re-layouts: 48.8 us -> 170 us
    unnamed x11 -> x140, local copies, waits for them, and re-layouts: 7.48 us -> 133 us
    reshape x1 -> x0, local copies, waits for them, and re-layouts: 5.4 us -> none  [shards(): blocks = pooled.reshape(tab_dev, devices, own_samples, feature_width)]
where the time goes in v1:
time: 344 us; the launch traced here: 338 us
  local copies, waits for them, and re-layouts  170 us (49%)
  other arithmetic  73.6 us (21%)
  waiting for transfers between devices  56.2 us (16%)
  matrix products  20.5 us (6%)
  starting transfers between devices  10.7 us (3%)
  loops' own time  7.11 us (2%)
    unnamed x140, local copies, waits for them, and re-layouts  133 us
    add x128, other arithmetic, add_ids(): return counts + hit.astype(jnp.bfloat16)  72.8 us
    all_to_all x1, waiting for transfers between devices, shards(): lax.all_to_all(row_out, axis_name=('hst', 'row', 'col'), split_axis=0, co...  56.2 us
    dot_general x32, matrix products, one_block(): jnp.dot(counts, table, preferred_element_type=jnp.float32)  15.7 us
    dynamic_slice x16, local copies, waits for them, and re-layouts, shards(): lax.map(lambda items: pool_table(items[0], items[1], items[2], bag_size),...  13.1 us
    all_to_all x1, starting transfers between devices, shards(): lax.all_to_all(row_out, axis_name=('hst', 'row', 'col'), split_axis=0, co...  10.7 us
    squeeze x8, local copies, waits for them, and re-layouts, shards(): lax.map(lambda items: pool_table(items[0], items[1], items[2], bag_size),...  7.73 us
  transfers between devices with their start and end apart: 1, of which 1 were waited for; matrix products, arithmetic and copies ran while one was open for 0% of the time, Pallas kernels for 0%

profile of v1, /device:TPU:34, one launch (start us, length us, event | category | flops | bytes accessed | tf_op | source)
XLA Modules:
  0.0 337.8 jit_solution(10602668357508147076)
XLA Ops:
  0.0 125.9 %while.38 = (s32[]{:T(128)}, bf16[8,2048,128]{2,1,0:T(8,128)(2,1)}, s32[8,2048,4]{1,2,0:T(4,128)}, s32[8,2048]{1,0:T(8,128)}, bf16[8,1024,128]{2,1,0:T(8,128)(2,...) while((s32[]{:T(128)}, bf16[8,2048,128]{2,1,0:T(8,128)(2,1)}, ...), condition=%wide.region_5.6_spmd, body=%wide.region_0.5_spmd.sunk | while | flops 138478080 | bytes 5248977 | solution.py:39
  2.6 12.3 %while.39 = (s32[]{:T(128)}, bf16[4,512,128]{2,1,0:T(8,128)(2,1)S(1)}, s32[4,512,4]{1,2,0:T(4,128)S(1)}, s32[4,512]{1,0:T(4,128)S(1)}, bf16[1024,128]{1,0:T(8,12...) while((s32[]{:T(128)}, bf16[4,512,128]{2,1,0:T(8,128)(2,1)S(1)}, ...), condition=%wide.region_4.4_spmd.clone, body=%wide.region_1.3_spmd.clone.sunk | while | flops 138478080 | bytes 3577096 | solution.py:28
  2.7 2.5 while.40
  5.8 2.5 while.40
  8.8 2.5 while.40
  11.9 2.5 while.40
  18.4 12.3 %while.39 = (s32[]{:T(128)}, bf16[4,512,128]{2,1,0:T(8,128)(2,1)S(1)}, s32[4,512,4]{1,2,0:T(4,128)S(1)}, s32[4,512]{1,0:T(4,128)S(1)}, bf16[1024,128]{1,0:T(8,12...) while((s32[]{:T(128)}, bf16[4,512,128]{2,1,0:T(8,128)(2,1)S(1)}, ...), condition=%wide.region_4.4_spmd.clone, body=%wide.region_1.3_spmd.clone.sunk | while | flops 138478080 | bytes 3577096 | solution.py:28
  18.4 2.5 while.40
  27.6 2.5 while.40
  34.1 12.3 %while.39 = (s32[]{:T(128)}, bf16[4,512,128]{2,1,0:T(8,128)(2,1)S(1)}, s32[4,512,4]{1,2,0:T(4,128)S(1)}, s32[4,512]{1,0:T(4,128)S(1)}, bf16[1024,128]{1,0:T(8,12...) while((s32[]{:T(128)}, bf16[4,512,128]{2,1,0:T(8,128)(2,1)S(1)}, ...), condition=%wide.region_4.4_spmd.clone, body=%wide.region_1.3_spmd.clone.sunk | while | flops 138478080 | bytes 3577096 | solution.py:28
  34.2 2.5 while.40
  40.3 2.5 while.40
  49.8 12.3 %while.39 = (s32[]{:T(128)}, bf16[4,512,128]{2,1,0:T(8,128)(2,1)S(1)}, s32[4,512,4]{1,2,0:T(4,128)S(1)}, s32[4,512]{1,0:T(4,128)S(1)}, bf16[1024,128]{1,0:T(8,12...) while((s32[]{:T(128)}, bf16[4,512,128]{2,1,0:T(8,128)(2,1)S(1)}, ...), condition=%wide.region_4.4_spmd.clone, body=%wide.region_1.3_spmd.clone.sunk | while | flops 138478080 | bytes 3577096 | solution.py:28
  56.0 2.5 while.40
  59.1 2.5 while.40
  65.6 12.3 %while.39 = (s32[]{:T(128)}, bf16[4,512,128]{2,1,0:T(8,128)(2,1)S(1)}, s32[4,512,4]{1,2,0:T(4,128)S(1)}, s32[4,512]{1,0:T(4,128)S(1)}, bf16[1024,128]{1,0:T(8,12...) while((s32[]{:T(128)}, bf16[4,512,128]{2,1,0:T(8,128)(2,1)S(1)}, ...), condition=%wide.region_4.4_spmd.clone, body=%wide.region_1.3_spmd.clone.sunk | while | flops 138478080 | bytes 3577096 | solution.py:28
  68.7 2.5 while.40
  71.8 2.5 while.40
  74.8 2.5 while.40
  81.3 12.3 %while.39 = (s32[]{:T(128)}, bf16[4,512,128]{2,1,0:T(8,128)(2,1)S(1)}, s32[4,512,4]{1,2,0:T(4,128)S(1)}, s32[4,512]{1,0:T(4,128)S(1)}, bf16[1024,128]{1,0:T(8,12...) while((s32[]{:T(128)}, bf16[4,512,128]{2,1,0:T(8,128)(2,1)S(1)}, ...), condition=%wide.region_4.4_spmd.clone, body=%wide.region_1.3_spmd.clone.sunk | while | flops 138478080 | bytes 3577096 | solution.py:28
  84.4 2.5 while.40
  97.0 12.3 %while.39 = (s32[]{:T(128)}, bf16[4,512,128]{2,1,0:T(8,128)(2,1)S(1)}, s32[4,512,4]{1,2,0:T(4,128)S(1)}, s32[4,512]{1,0:T(4,128)S(1)}, bf16[1024,128]{1,0:T(8,12...) while((s32[]{:T(128)}, bf16[4,512,128]{2,1,0:T(8,128)(2,1)S(1)}, ...), condition=%wide.region_4.4_spmd.clone, body=%wide.region_1.3_spmd.clone.sunk | while | flops 138478080 | bytes 3577096 | solution.py:28
  103.2 2.5 while.40
  106.3 2.5 while.40
  112.8 12.3 %while.39 = (s32[]{:T(128)}, bf16[4,512,128]{2,1,0:T(8,128)(2,1)S(1)}, s32[4,512,4]{1,2,0:T(4,128)S(1)}, s32[4,512]{1,0:T(4,128)S(1)}, bf16[1024,128]{1,0:T(8,12...) while((s32[]{:T(128)}, bf16[4,512,128]{2,1,0:T(8,128)(2,1)S(1)}, ...), condition=%wide.region_4.4_spmd.clone, body=%wide.region_1.3_spmd.clone.sunk | while | flops 138478080 | bytes 3577096 | solution.py:28
  112.8 2.5 while.40
  122.0 2.5 while.40
  252.1 10.7 %all-to-all-start = ((bf16[128,8,1,16,128]{4,3,1,2,0:T(8,128)(2,1)}), bf16[128,8,1,16,128]{4,3,1,2,0:T(8,128)(2,1)}, u32[]{:S(2)}, u32[]{:S(2)}) async-start(bf16[128,8,1,16,128]{4,3,1,2,0:T(8,128)(2,1)} %constant_dynamic-update-slice_fusion.2), calls=%async_computation | async-start | bytes 8388608 | tf_op jit(solution)/shard_map/all_to_all | solution.py:55
  262.9 56.2 %all-to-all-done = bf16[128,8,1,16,128]{4,3,1,2,0:T(8,128)(2,1)} async-done(((bf16[128,8,1,16,128]{4,3,1,2,0:T(8,128)(2,1)}), bf16[128,8,1,16,128]{4,3,1,2,0:T(8,128)(2,1)}, u32[]{:S(2)}, u32[]{:S(2)}) %all-to-all-start) | async-done | bytes 4194336 | tf_op jit(solution)/shard_map/all_to_all | solution.py:55
  319.2 6.3 %copy.525 = bf16[128,8,16,128]{3,1,2,0:T(8,128)(2,1)} copy(bf16[128,8,16,128]{3,2,1,0:T(8,128)(2,1)} %bitcast.397) | data formatting | bytes 8388608
  325.5 6.4 %copy.393 = bf16[2048,1024]{1,0:T(8,128)(2,1)} copy(bf16[2048,1024]{0,1:T(8,128)(2,1)} %bitcast.827) | data formatting | bytes 8388608 | tf_op jit(solution)/shard_map/dot_general | solution.py:59
  331.9 4.4 %add_convert_fusion = bf16[256,16,128]{2,0,1:T(8,128)(2,1)S(1)} fusion(bf16[16,128,1024]{2,1,0:T(8,128)(2,1)} %bitcast.829, f32[16,128]{1,0:T(8,128)S(1)} %convert_element_type.40, f32[256]{0:T(256)S(1)} %bitcast.960, s32[1024]{0:T(1024)S(1)} %fusion.29, s32[1024]{0:T(1024)S(1)} %copy-done.4, bf16[256,1025]{0,1:T(8,128)(2,1)S(1)} %constant_dynamic-update-slice_fusion), kind=kOutput, calls=%fused_computation.17 | convolution fusion | flops 1613496320 | bytes 5784576 | tf_op jit(solution)/shard_map/dot_general | solution.py:59
  (752 shorter events, 281.5 us)
Async XLA Ops:
  125.9 87.4 %copy-start = (bf16[8,2048,128]{2,1,0:T(8,128)(2,1)S(1)}, bf16[8,2048,128]{2,1,0:T(8,128)(2,1)}, u32[]{:S(2)}) copy-start(bf16[8,2048,128]{2,1,0:T(8,128)(2,1)} %get-tuple-element.158) | copy-start | bytes 12582916
  252.1 10.7 %copy-start.3 = (bf16[16,128]{1,0:T(8,128)(2,1)S(1)}, bf16[16,128]{1,0:T(8,128)(2,1)}, u32[]{:S(2)}) copy-start(bf16[16,128]{1,0:T(8,128)(2,1)} %param.17) | copy-start | bytes 12292
  252.1 10.7 %copy-start.1 = (bf16[128,1025]{0,1:T(8,128)(2,1)S(1)}, bf16[128,1025]{0,1:T(8,128)(2,1)}, u32[]{:S(2)}) copy-start(bf16[128,1025]{0,1:T(8,128)(2,1)} %param.18) | copy-start | bytes 787204
  252.1 10.8 %copy-start.2 = (bf16[128,1025]{0,1:T(8,128)(2,1)S(1)}, bf16[128,1025]{0,1:T(8,128)(2,1)}, u32[]{:S(2)}) copy-start(bf16[128,1025]{0,1:T(8,128)(2,1)} %param.19) | copy-start | bytes 787204
  252.1 67.1 %all-to-all-start = ((bf16[128,8,1,16,128]{4,3,1,2,0:T(8,128)(2,1)}), bf16[128,8,1,16,128]{4,3,1,2,0:T(8,128)(2,1)}, u32[]{:S(2)}, u32[]{:S(2)}) async-start(bf16[128,8,1,16,128]{4,3,1,2,0:T(8,128)(2,1)} %constant_dynamic-update-slice_fusion.2), calls=%async_computation | async-start | bytes 8388608 | tf_op jit(solution)/shard_map/all_to_all | solution.py:55
  325.5 6.4 %copy-start.4 = (s32[1024]{0:T(1024)S(1)}, s32[1024]{0:T(1024)}, u32[]{:S(2)}) copy-start(s32[1024]{0:T(1024)} %param.16) | copy-start | bytes 12292
